TPU v7x, 32 devices: a whole 2x2x4 slice. The times are simulated.
32 devices in a mesh: row: 4 (over x, core), col: 8 (over z, y).
Axes of the slice: x: 2, y: 2, z: 4, core: 2. Of those that a mesh axis runs over, the one named last changes fastest.
Arguments:
- tiles: int32 [4, 8, 8, 128, 128], P('row', 'col'), may hold values from 0 to 1073741823, as said below
- slots: int32 [4, 8, 8], P('row', 'col'), may hold values from 0 to 31, as said below
- factor: float32 [4096, 256], P(('row', 'col')), may hold values from -0.5 to 0.5
- dual: float32 [4096, 256], P(('row', 'col')), may hold values from -0.5 to 0.5
Outputs:
- final_factor: float32 [4096, 256], P(('row', 'col'))
- final_dual: float32 [4096, 256], P(('row', 'col'))
- objective: float32 [3], replicated
- residual: float32 [3], replicated
Inputs may be any that keep to these rules, and one draw needn't show every extreme that they name: `slots`: for every device, 8 distinct block numbers in ascending order. The stored blocks of all devices form a symmetric pattern: the block of rows piece p and columns piece q is stored if and only if the block of rows piece q and columns piece p is; every diagonal block is stored. `tiles`: the stored block of rows piece p and columns piece q is the transpose of the one of rows piece q and columns piece p; diagonal blocks are symmetric.
All inputs are finite; a program needn't handle non-finite values.
Results may differ from a plain program's by a relative error of at most 0.005.
Values may be sent and summed in bfloat16 or wider, within the bound.
A program may use at most 64 MiB of HBM per device.

v0:
```python
import math
import jax
import jax.numpy as jnp
from jax import lax
from jax.sharding import PartitionSpec as P

ITERS = 3
penalty = 2.0
step_size = 0.25
ridge_shift = 0.1
offset = 536870912


def block_weights(integers, vertices):
    unit_scale = math.sqrt(6.0 / vertices) / 2.0**29
    return ((integers - offset).astype(jnp.float32) * unit_scale).astype(jnp.bfloat16)


def unit_rows(values):
    return values * lax.rsqrt(jnp.sum(values * values, axis=1, keepdims=True) + 1e-06)


def local(tiles, slots, factor, dual):
    row_count = lax.axis_size("row")
    col_count = lax.axis_size("col")
    piece_rows = factor.shape[0]
    columns = factor.shape[1]
    vertices = piece_rows * row_count * col_count
    weights = block_weights(tiles.reshape(tiles.shape[2], piece_rows, piece_rows), vertices)
    stored = slots.reshape(-1)
    block_row = stored // row_count
    block_col = stored % row_count

    def combine(partial_value):
        return lax.psum_scatter(partial_value, "col", scatter_dimension=0, tiled=True)

    selector = (block_row[None, :] == jnp.arange(col_count, dtype=jnp.int32)[:, None]).astype(
        jnp.float32
    )
    block_sums = jnp.sum(weights, axis=2, dtype=jnp.float32)
    edge_sums = jnp.dot(selector, block_sums, precision=lax.Precision.HIGHEST)
    degree = combine(edge_sums.reshape(-1))
    current = factor
    lagrange = dual
    projected = unit_rows(current + lagrange / penalty)
    tallies = []
    for iteration in range(ITERS):
        packed = current.astype(jnp.bfloat16)
        own_gram = lax.dot_general(
            packed, packed, (((0,), (0,)), ((), ())), preferred_element_type=jnp.float32
        )
        gram_total = lax.psum(own_gram, ("row", "col"))
        gathered = lax.all_gather(packed, "row", axis=0, tiled=True).reshape(
            -1, piece_rows, columns
        )
        chosen = gathered[block_col]
        products = jnp.einsum("tij,tjk->tik", weights, chosen, preferred_element_type=jnp.float32)
        partial_value = jnp.einsum(
            "at,tik->aik", selector, products, precision=lax.Precision.HIGHEST
        )
        coupled = combine(partial_value.reshape(col_count * piece_rows, columns))
        widened = packed.astype(jnp.float32)
        gradient = degree[:, None] * widened - coupled
        precond = columns / vertices * gram_total + ridge_shift * jnp.eye(
            columns, dtype=jnp.float32
        )
        triangle = jnp.linalg.cholesky(precond)
        descent = 2.0 * gradient - lagrange - penalty * (current - projected)
        current = current + step_size * jax.scipy.linalg.cho_solve((triangle, True), descent.T).T
        projected = unit_rows(current + lagrange / penalty)
        lagrange = lagrange + penalty * (current - projected)
        mismatch = current - projected
        local_sums = jnp.stack([jnp.sum(widened * gradient), jnp.sum(mismatch * mismatch)])
        tallies.append(local_sums)
    stacked = jnp.stack(tallies)
    stacked = lax.psum(stacked, ("row", "col"))
    objective = stacked[:, 0] / (4.0 * vertices)
    residual = stacked[:, 1] / vertices
    return (current, lagrange, objective, residual)


def solution(mesh):
    in_specs = (
        P("row", "col", None, None, None),
        P("row", "col", None),
        P(("row", "col"), None),
        P(("row", "col"), None),
    )
    out_specs = (P(("row", "col"), None), P(("row", "col"), None), P(), P())
    return jax.shard_map(local, mesh=mesh, in_specs=in_specs, out_specs=out_specs, check_vma=False)
```

profile of v0, /device:TPU:0, one launch (start us, length us, event | category | flops | bytes accessed | tf_op | source)
XLA Modules:
  0.0 669.2 jit_solution(12461409791366380685)
XLA Ops:
  10.2 7.2 %all_gather.9 = bf16[512,256]{0,1:T(8,128)(2,1)S(1)} all-gather(bf16[128,256]{0,1:T(8,128)(2,1)S(1)} %get-tuple-element.92), channel_id=1, replica_groups=mesh['row'=4,'col'=8] {'row'}, dimensions={0}, use_global_device_ids=true | all-gather | bytes 327680 | tf_op jit(solution)/shard_map/all_gather | solution.py:53
  21.8 22.3 %all-reduce.1 = f32[1024]{0:T(1024)S(1)} all-reduce(f32[1024]{0:T(1024)S(1)} %convolution_bitcast_fusion), channel_id=2, replica_groups=mesh['row'=4,'col'=8] {'col'}, use_global_device_ids=true, to_apply=%region_6.8.clone | all-reduce | flops 1024 | bytes 8192
  46.1 99.0 %all-reduce.6.cloned.1.call-done = f32[256,256]{0,1:T(8,128)} async-done(((f32[256,256]{0,1:T(8,128)}), f32[256,256]{0,1:T(8,128)}) %all-reduce.6.cloned.1.call-update) | async-done | bytes 262160 | tf_op jit(solution)/shard_map/psum | solution.py:52
  147.1 11.7 %cholesky.172 = f32[128,128]{1,0:T(8,128)S(1)} custom-call(f32[128,128]{1,0:T(8,128)S(1)} %cholesky.270), custom_call_target="Cholesky" | custom-call | tf_op jit(solution)/shard_map/jit(cholesky)/cholesky | solution.py:67
  158.9 9.8 %custom-call.17 = f32[1,128,128]{1,2,0:T(8,128)S(1)} custom-call(f32[1,128,128]{2,1,0:T(8,128)S(1)} %get-tuple-element.104), custom_call_target="InvertDiagBlocksLowerTriangular" | custom-call | tf_op jit(solution)/shard_map/jit(cholesky)/cholesky | solution.py:67
  169.2 11.7 %cholesky.189 = f32[128,128]{1,0:T(8,128)S(1)} custom-call(f32[128,128]{1,0:T(8,128)S(1)} %convolution_subtract_fusion.8), custom_call_target="Cholesky" | custom-call | tf_op jit(solution)/shard_map/jit(cholesky)/cholesky | solution.py:67
  183.0 4.2 while.6
  187.2 19.7 %custom-call.18 = f32[2,128,128]{1,2,0:T(8,128)S(1)} custom-call(f32[2,128,128]{2,1,0:T(8,128)S(1)} %get-tuple-element.26), custom_call_target="InvertDiagBlocksLowerTriangular" | custom-call | tf_op jit(solution)/shard_map/jit(_cho_solve)/triangular_solve | solution.py:69
  209.4 5.8 all_gather.10
  220.1 126.6 %all-reduce.8.cloned.1.call-done = f32[256,256]{0,1:T(8,128)} async-done(((f32[256,256]{0,1:T(8,128)}), f32[256,256]{0,1:T(8,128)}) %all-reduce.8.cloned.1.call-update) | async-done | bytes 262160 | tf_op jit(solution)/shard_map/psum | solution.py:52
  348.7 11.7 %cholesky.206 = f32[128,128]{1,0:T(8,128)S(1)} custom-call(f32[128,128]{1,0:T(8,128)S(1)} %cholesky.273), custom_call_target="Cholesky" | custom-call | tf_op jit(solution)/shard_map/jit(cholesky)/cholesky | solution.py:67
  360.4 9.8 %custom-call.19 = f32[1,128,128]{1,2,0:T(8,128)S(1)} custom-call(f32[1,128,128]{2,1,0:T(8,128)S(1)} %get-tuple-element.100), custom_call_target="InvertDiagBlocksLowerTriangular" | custom-call | tf_op jit(solution)/shard_map/jit(cholesky)/cholesky | solution.py:67
  370.7 11.7 %cholesky.223 = f32[128,128]{1,0:T(8,128)S(1)} custom-call(f32[128,128]{1,0:T(8,128)S(1)} %convolution_subtract_fusion.5), custom_call_target="Cholesky" | custom-call | tf_op jit(solution)/shard_map/jit(cholesky)/cholesky | solution.py:67
  385.1 4.2 while.7
  389.3 19.7 %custom-call.20 = f32[2,128,128]{1,2,0:T(8,128)S(1)} custom-call(f32[2,128,128]{2,1,0:T(8,128)S(1)} %get-tuple-element.27), custom_call_target="InvertDiagBlocksLowerTriangular" | custom-call | tf_op jit(solution)/shard_map/jit(_cho_solve)/triangular_solve | solution.py:69
  413.1 5.8 all_gather.11
  422.7 126.8 %all-reduce.10.cloned.1.call-done = f32[256,256]{0,1:T(8,128)} async-done(((f32[256,256]{0,1:T(8,128)}), f32[256,256]{0,1:T(8,128)}) %all-reduce.10.cloned.1.call-update) | async-done | bytes 262160 | tf_op jit(solution)/shard_map/psum | solution.py:52
  551.5 11.7 %cholesky.240 = f32[128,128]{1,0:T(8,128)S(1)} custom-call(f32[128,128]{1,0:T(8,128)S(1)} %cholesky.276), custom_call_target="Cholesky" | custom-call | tf_op jit(solution)/shard_map/jit(cholesky)/cholesky | solution.py:67
  563.3 9.8 %custom-call.21 = f32[1,128,128]{1,2,0:T(8,128)S(1)} custom-call(f32[1,128,128]{2,1,0:T(8,128)S(1)} %get-tuple-element.96), custom_call_target="InvertDiagBlocksLowerTriangular" | custom-call | tf_op jit(solution)/shard_map/jit(cholesky)/cholesky | solution.py:67
  573.6 11.7 %cholesky.257 = f32[128,128]{1,0:T(8,128)S(1)} custom-call(f32[128,128]{1,0:T(8,128)S(1)} %convolution_subtract_fusion.2), custom_call_target="Cholesky" | custom-call | tf_op jit(solution)/shard_map/jit(cholesky)/cholesky | solution.py:67
  588.0 4.3 while.8
  592.3 19.7 %custom-call.22 = f32[2,128,128]{1,2,0:T(8,128)S(1)} custom-call(f32[2,128,128]{2,1,0:T(8,128)S(1)} %get-tuple-element.28), custom_call_target="InvertDiagBlocksLowerTriangular" | custom-call | tf_op jit(solution)/shard_map/jit(_cho_solve)/triangular_solve | solution.py:69
  612.0 1.7 fusion.7
  621.5 39.2 %psum.31 = f32[3,2]{1,0:T(4,128)S(1)} all-reduce(f32[3,2]{1,0:T(4,128)S(1)} %pad_maximum_fusion), channel_id=1, replica_groups=mesh['row'=4,'col'=8] {'row','col'}, use_global_device_ids=true, to_apply=%region_22.25 | all-reduce | flops 6 | bytes 48 | tf_op jit(solution)/shard_map/psum | solution.py:76
  (159 shorter events, 54.2 us)
Async XLA Ops:
  8.0 1.1 copy-start.6
  8.0 137.1 %all-reduce.6.cloned.1.call-start = ((), (), s32[]{:S(2)}) async-start(), calls=%async_computation.3 | async-start | bytes 524288 | tf_op jit(solution)/shard_map/psum | solution.py:52
  9.2 8.3 %copy-start.4 = (s32[1,1,8,128,128]{4,3,2,1,0:T(8,128)S(1)}, s32[1,1,8,128,128]{4,3,2,1,0:T(8,128)}, u32[]{:S(2)}) copy-start(s32[1,1,8,128,128]{4,3,2,1,0:T(8,128)} %param.7) | copy-start | bytes 1572868
  10.2 7.3 %copy-start.7 = (s32[1,1,8]{2,1,0:T(1,128)S(1)}, s32[1,1,8]{2,1,0:T(1,128)}, u32[]{:S(2)}) copy-start(s32[1,1,8]{2,1,0:T(1,128)} %param.8) | copy-start | bytes 100
  10.2 196.7 %reduce-scatter.4.cloned.1.call-start = ((), (), s32[]{:S(2)}) async-start(), calls=%async_computation.4 | async-start | bytes 1179648 | tf_op jit(solution)/shard_map/reduce_scatter | solution.py:35
  21.6 325.0 %all-reduce.8.cloned.1.call-start = ((), (), s32[]{:S(2)}) async-start(), calls=%async_computation.5 | async-start | bytes 524288 | tf_op jit(solution)/shard_map/psum | solution.py:52
  44.1 0.7 copy-start.8
  146.1 1.0 copy-start
  219.4 189.6 %reduce-scatter.6.cloned.1.call-start = ((), (), s32[]{:S(2)}) async-start(), calls=%async_computation.6 | async-start | bytes 1179648 | tf_op jit(solution)/shard_map/reduce_scatter | solution.py:35
  220.0 329.5 %all-reduce.10.cloned.1.call-start = ((), (), s32[]{:S(2)}) async-start(), calls=%async_computation.7 | async-start | bytes 524288 | tf_op jit(solution)/shard_map/psum | solution.py:52
  347.6 1.0 copy-start.1
  422.2 189.8 %reduce-scatter.8.cloned.1.call-start = ((), (), s32[]{:S(2)}) async-start(), calls=%async_computation.8 | async-start | bytes 1179648 | tf_op jit(solution)/shard_map/reduce_scatter | solution.py:35
  550.5 1.0 copy-start.2
  587.9 24.1 %copy-start.5 = (f32[128,256]{0,1:T(8,128)S(1)}, f32[128,256]{0,1:T(8,128)}, u32[]{:S(2)}) copy-start(f32[128,256]{0,1:T(8,128)} %reduce-scatter.4.cloned.1.call-done) | copy-start | bytes 393220
  588.0 24.0 %copy-start.3 = (f32[128,256]{0,1:T(8,128)S(1)}, f32[128,256]{0,1:T(8,128)}, u32[]{:S(2)}) copy-start(f32[128,256]{0,1:T(8,128)} %reduce-scatter.6.cloned.1.call-done) | copy-start | bytes 393220
Sparse Core Ops, SparseCore 0:
  14.3 130.7 all-reduce.5
  219.5 127.0 all-reduce.7
  422.3 127.1 all-reduce.9
Sparse Core Ops, SparseCore 1:
  21.7 66.1 reduce-scatter.3
  223.3 63.7 reduce-scatter.5
  426.0 63.8 reduce-scatter.7
where the time goes:
time: 673 us; the launch traced here: 669 us
  waiting for transfers between devices  354 us (53%)
  other arithmetic  176 us (26%)
  blocking collectives  80.4 us (12%)
  local copies, waits for them, and re-layouts  25.8 us (4%)
  between operations  21.1 us (3%)
  matrix products  11.9 us (2%)
    psum x3, waiting for transfers between devices, local(): gram_total = lax.psum(own_gram, ('row', 'col'))  352 us
    another operation x20, other arithmetic, local(): triangle = jnp.linalg.cholesky(precond)  103 us
    another operation x7, other arithmetic, local(): jax.scipy.linalg.cho_solve((triangle, True), descent.T)  59.1 us
    psum x1, blocking collectives, local(): stacked = lax.psum(stacked, ('row', 'col'))  39.2 us
    unnamed x1, blocking collectives  22.3 us
    all_gather x3, blocking collectives, local(): lax.all_gather(packed, 'row', axis=0, tiled=True)  18.8 us
  transfers between devices with their start and end apart: 6, of which 3 were waited for; matrix products, arithmetic and copies ran while one was open for 27% of the time, Pallas kernels for 0%

commit v1 on v0

--- a/solution.py
+++ b/solution.py
@@ -49,7 +49,7 @@
         own_gram = lax.dot_general(
             packed, packed, (((0,), (0,)), ((), ())), preferred_element_type=jnp.float32
         )
-        gram_total = lax.psum(own_gram, ("row", "col"))
+        gram_total = jnp.sum(lax.all_gather(own_gram, ("row", "col")), axis=0)
         gathered = lax.all_gather(packed, "row", axis=0, tiled=True).reshape(
             -1, piece_rows, columns
         )

time: 673 us -> 559 us (0.83)
  waiting for transfers between devices: 354 us -> 231 us
  other arithmetic: 176 us -> 187 us
    psum x3 -> x0, waiting for transfers between devices: 352 us -> none  [local(): gram_total = lax.psum(own_gram, ('row', 'col'))]
    reduce_scatter x3, waiting for transfers between devices: 0.08 us -> 231 us  [combine(): lax.psum_scatter(partial_value, 'col', scatter_dimension=0, tiled=True)]
    reduce_sum x0 -> x3, other arithmetic: none -> 11.8 us  [local(): gram_total = jnp.sum(lax.all_gather(own_gram, ('row', 'col')), axis=0)]
  transfers between devices with their start and end apart: 6 -> 6, of which waited for: 3 -> 3; matrix products, arithmetic and copies ran while one was open for 27% -> 2% of each run, Pallas kernels for 0% -> 0%
where the time goes in v1:
time: 559 us; the launch traced here: 555 us
  waiting for transfers between devices  231 us (41%)
  other arithmetic  187 us (33%)
  blocking collectives  79.3 us (14%)
  local copies, waits for them, and re-layouts  24.3 us (4%)
  between operations  20.9 us (4%)
  matrix products  11.8 us (2%)
    reduce_scatter x3, waiting for transfers between devices, combine(): lax.psum_scatter(partial_value, 'col', scatter_dimension=0, tiled=True)  231 us
    another operation x20, other arithmetic, local(): triangle = jnp.linalg.cholesky(precond)  103 us
    another operation x7, other arithmetic, local(): jax.scipy.linalg.cho_solve((triangle, True), descent.T)  59.1 us
    psum x1, blocking collectives, local(): stacked = lax.psum(stacked, ('row', 'col'))  38 us
    unnamed x1, blocking collectives  22.4 us
    all_gather x3, blocking collectives, local(): lax.all_gather(packed, 'row', axis=0, tiled=True)  18.9 us
    another operation x22, local copies, waits for them, and re-layouts, local(): jax.scipy.linalg.cho_solve((triangle, True), descent.T)  12.1 us
    reduce_sum x3, other arithmetic, local(): gram_total = jnp.sum(lax.all_gather(own_gram, ('row', 'col')), axis=0)  11.8 us
  transfers between devices with their start and end apart: 6, of which 3 were waited for; matrix products, arithmetic and copies ran while one was open for 2% of the time, Pallas kernels for 0%

profile of v1, /device:TPU:0, one launch (start us, length us, event | category | flops | bytes accessed | tf_op | source)
XLA Modules:
  0.0 555.5 jit_solution(6155257905949352195)
XLA Ops:
  11.4 7.2 %all_gather.29 = bf16[512,256]{0,1:T(8,128)(2,1)S(1)} all-gather(bf16[128,256]{0,1:T(8,128)(2,1)S(1)} %get-tuple-element.92), channel_id=1, replica_groups=mesh['row'=4,'col'=8] {'row'}, dimensions={0}, use_global_device_ids=true | all-gather | bytes 327680 | tf_op jit(solution)/shard_map/all_gather | solution.py:53
  26.3 22.4 %all-reduce.1 = f32[1024]{0:T(1024)S(1)} all-reduce(f32[1024]{0:T(1024)S(1)} %convolution_bitcast_fusion), channel_id=5, replica_groups=mesh['row'=4,'col'=8] {'col'}, use_global_device_ids=true, to_apply=%region_6.8.clone | all-reduce | flops 1024 | bytes 8192
  48.8 62.7 %reduce-scatter.4.cloned.1.call-done = f32[128,256]{0,1:T(8,128)} async-done(((f32[1024,256]{0,1:T(8,128)}), f32[128,256]{0,1:T(8,128)}) %reduce-scatter.4.cloned.1.call-update) | async-done | bytes 131088 | tf_op jit(solution)/shard_map/reduce_scatter | solution.py:35
  112.5 3.9 reduce_sum.126
  116.8 11.7 %cholesky.172 = f32[128,128]{1,0:T(8,128)S(1)} custom-call(f32[128,128]{1,0:T(8,128)S(1)} %cholesky.270), custom_call_target="Cholesky" | custom-call | tf_op jit(solution)/shard_map/jit(cholesky)/cholesky | solution.py:67
  128.6 9.8 %custom-call.17 = f32[1,128,128]{1,2,0:T(8,128)S(1)} custom-call(f32[1,128,128]{2,1,0:T(8,128)S(1)} %get-tuple-element.104), custom_call_target="InvertDiagBlocksLowerTriangular" | custom-call | tf_op jit(solution)/shard_map/jit(cholesky)/cholesky | solution.py:67
  138.9 11.7 %cholesky.189 = f32[128,128]{1,0:T(8,128)S(1)} custom-call(f32[128,128]{1,0:T(8,128)S(1)} %convolution_subtract_fusion.8), custom_call_target="Cholesky" | custom-call | tf_op jit(solution)/shard_map/jit(cholesky)/cholesky | solution.py:67
  152.7 4.2 while.6
  156.9 19.7 %custom-call.18 = f32[2,128,128]{1,2,0:T(8,128)S(1)} custom-call(f32[2,128,128]{2,1,0:T(8,128)S(1)} %get-tuple-element.26), custom_call_target="InvertDiagBlocksLowerTriangular" | custom-call | tf_op jit(solution)/shard_map/jit(_cho_solve)/triangular_solve | solution.py:69
  178.1 5.9 %all_gather.32 = bf16[512,256]{0,1:T(8,128)(2,1)S(1)} all-gather(bf16[128,256]{0,1:T(8,128)(2,1)S(1)} %get-tuple-element.78), channel_id=1, replica_groups=mesh['row'=4,'col'=8] {'row'}, dimensions={0}, use_global_device_ids=true | all-gather | bytes 327680 | tf_op jit(solution)/shard_map/all_gather | solution.py:53
  188.4 84.3 %reduce-scatter.6.cloned.1.call-done = f32[128,256]{0,1:T(8,128)} async-done(((f32[1024,256]{0,1:T(8,128)}), f32[128,256]{0,1:T(8,128)}) %reduce-scatter.6.cloned.1.call-update) | async-done | bytes 131088 | tf_op jit(solution)/shard_map/reduce_scatter | solution.py:35
  278.6 11.7 %cholesky.206 = f32[128,128]{1,0:T(8,128)S(1)} custom-call(f32[128,128]{1,0:T(8,128)S(1)} %cholesky.273), custom_call_target="Cholesky" | custom-call | tf_op jit(solution)/shard_map/jit(cholesky)/cholesky | solution.py:67
  290.4 9.8 %custom-call.19 = f32[1,128,128]{1,2,0:T(8,128)S(1)} custom-call(f32[1,128,128]{2,1,0:T(8,128)S(1)} %get-tuple-element.100), custom_call_target="InvertDiagBlocksLowerTriangular" | custom-call | tf_op jit(solution)/shard_map/jit(cholesky)/cholesky | solution.py:67
  300.7 11.7 %cholesky.223 = f32[128,128]{1,0:T(8,128)S(1)} custom-call(f32[128,128]{1,0:T(8,128)S(1)} %convolution_subtract_fusion.5), custom_call_target="Cholesky" | custom-call | tf_op jit(solution)/shard_map/jit(cholesky)/cholesky | solution.py:67
  315.2 4.5 while.7
  319.7 19.7 %custom-call.20 = f32[2,128,128]{1,2,0:T(8,128)S(1)} custom-call(f32[2,128,128]{2,1,0:T(8,128)S(1)} %get-tuple-element.27), custom_call_target="InvertDiagBlocksLowerTriangular" | custom-call | tf_op jit(solution)/shard_map/jit(_cho_solve)/triangular_solve | solution.py:69
  340.9 5.8 %all_gather.35 = bf16[512,256]{0,1:T(8,128)(2,1)S(1)} all-gather(bf16[128,256]{0,1:T(8,128)(2,1)S(1)} %convert_element_type.43), channel_id=1, replica_groups=mesh['row'=4,'col'=8] {'row'}, dimensions={0}, use_global_device_ids=true | all-gather | bytes 327680 | tf_op jit(solution)/shard_map/all_gather | solution.py:53
  351.1 84.0 %reduce-scatter.8.cloned.1.call-done = f32[128,256]{0,1:T(8,128)} async-done(((f32[1024,256]{0,1:T(8,128)}), f32[128,256]{0,1:T(8,128)}) %reduce-scatter.8.cloned.1.call-update) | async-done | bytes 131088 | tf_op jit(solution)/shard_map/reduce_scatter | solution.py:35
  442.4 11.7 %cholesky.240 = f32[128,128]{1,0:T(8,128)S(1)} custom-call(f32[128,128]{1,0:T(8,128)S(1)} %cholesky.276), custom_call_target="Cholesky" | custom-call | tf_op jit(solution)/shard_map/jit(cholesky)/cholesky | solution.py:67
  454.2 9.8 %custom-call.21 = f32[1,128,128]{1,2,0:T(8,128)S(1)} custom-call(f32[1,128,128]{2,1,0:T(8,128)S(1)} %get-tuple-element.96), custom_call_target="InvertDiagBlocksLowerTriangular" | custom-call | tf_op jit(solution)/shard_map/jit(cholesky)/cholesky | solution.py:67
  464.5 11.7 %cholesky.257 = f32[128,128]{1,0:T(8,128)S(1)} custom-call(f32[128,128]{1,0:T(8,128)S(1)} %convolution_subtract_fusion.2), custom_call_target="Cholesky" | custom-call | tf_op jit(solution)/shard_map/jit(cholesky)/cholesky | solution.py:67
  478.9 4.2 while.8
  483.0 19.7 %custom-call.22 = f32[2,128,128]{1,2,0:T(8,128)S(1)} custom-call(f32[2,128,128]{2,1,0:T(8,128)S(1)} %get-tuple-element.28), custom_call_target="InvertDiagBlocksLowerTriangular" | custom-call | tf_op jit(solution)/shard_map/jit(_cho_solve)/triangular_solve | solution.py:69
  508.5 38.0 %psum.7 = f32[3,2]{1,0:T(4,128)S(1)} all-reduce(f32[3,2]{1,0:T(4,128)S(1)} %pad_maximum_fusion), channel_id=1, replica_groups=mesh['row'=4,'col'=8] {'row','col'}, use_global_device_ids=true, to_apply=%region_22.25 | all-reduce | flops 6 | bytes 48 | tf_op jit(solution)/shard_map/psum | solution.py:76
  (153 shorter events, 60.8 us)
Async XLA Ops:
  8.0 17.0 %copy-start.2 = (u32[32]{0:T(128)S(1)}, u32[32]{0:T(128)}, u32[]{:S(2)}) copy-start(u32[32]{0:T(128)} %constant.153) | copy-start | bytes 388
  8.0 103.5 %reduce-scatter.4.cloned.1.call-start = ((), (), s32[]{:S(2)}) async-start(), calls=%async_computation.3 | async-start | bytes 1179648 | tf_op jit(solution)/shard_map/reduce_scatter | solution.py:35
  23.9 88.6 %all-gather.7.cloned.1.call-start = ((), (), s32[]{:S(2)}) async-start(), calls=%async_computation.6 | async-start | bytes 8650752 | tf_op jit(solution)/shard_map/all_gather | solution.py:52
  24.9 247.8 %reduce-scatter.6.cloned.1.call-start = ((), (), s32[]{:S(2)}) async-start(), calls=%async_computation.4 | async-start | bytes 1179648 | tf_op jit(solution)/shard_map/reduce_scatter | solution.py:35
  187.3 87.0 %all-gather.9.cloned.1.call-start = ((), (), s32[]{:S(2)}) async-start(), calls=%async_computation.7 | async-start | bytes 8650752 | tf_op jit(solution)/shard_map/all_gather | solution.py:52
  188.3 246.8 %reduce-scatter.8.cloned.1.call-start = ((), (), s32[]{:S(2)}) async-start(), calls=%async_computation.5 | async-start | bytes 1179648 | tf_op jit(solution)/shard_map/reduce_scatter | solution.py:35
  278.5 156.5 %copy-start = (f32[128,256]{0,1:T(8,128)S(1)}, f32[128,256]{0,1:T(8,128)}, u32[]{:S(2)}) copy-start(f32[128,256]{0,1:T(8,128)} %reduce-scatter.6.cloned.1.call-done) | copy-start | bytes 393220
  278.6 156.5 %copy-start.1 = (f32[128,256]{0,1:T(8,128)S(1)}, f32[128,256]{0,1:T(8,128)}, u32[]{:S(2)}) copy-start(f32[128,256]{0,1:T(8,128)} %reduce-scatter.4.cloned.1.call-done) | copy-start | bytes 393220
  350.1 88.0 %all-gather.11.cloned.1.call-start = ((), (), s32[]{:S(2)}) async-start(), calls=%async_computation.8 | async-start | bytes 8650752 | tf_op jit(solution)/shard_map/all_gather | solution.py:52
Sparse Core Ops, SparseCore 0:
  24.0 87.4 reduce-scatter.3
  187.4 85.2 reduce-scatter.5
  350.2 84.7 reduce-scatter.7
Sparse Core Ops, SparseCore 1:
  27.4 80.0 all-gather.6
  190.8 77.8 all-gather.8
  353.6 77.7 all-gather.10
